TPU v7x, 512 devices: a whole 4x4x16 slice. The times are simulated.
512 devices in a mesh: dp: 128 (over y, x_lo, z), shard: 4 (over x_hi, core).
Axes of the slice: x: 4 (x_hi: 2, x_lo: 2; x = x_hi * 2 + x_lo), y: 4, z: 16, core: 2. Of those that a mesh axis runs over, the one named last changes fastest.
Arguments:
- hidden_acts: bfloat16 [128, 128, 8192], P('dp', None, 'shard'), may hold values from -6 to 6
- out_grad: bfloat16 [128, 128, 1024], P('dp'), may hold values from -0.0546875 to 0.0546875
- token_ids: int32 [128, 128], P('dp'), may hold values from 0 to 255999, as said below
- trigger: int32 [128, 512], P('dp', 'shard'), may hold values 0 or 1
- stale: bfloat16 [128, 8192, 1024], P('dp', 'shard'), may hold values from -0.5 to 0.5
- aggregate_prev: float32 [4, 2048, 1024], P('shard', 'dp'), may hold values from -12 to 12
Outputs:
- aggregate: float32 [4, 2048, 1024], P('shard', 'dp')
- update: float32 [4, 2048, 1024], P('shard', 'dp')
- triggered: float32 [], replicated
Inputs may be any that keep to these rules, and one draw needn't show every extreme that they name: `token_ids`: id 0 marks padding and stands only after all of a worker's other tokens; at least half of each worker's 128 tokens are not padding.
All inputs are finite; a program needn't handle non-finite values. No bound on the sum of `trigger` on one device may be relied on, other than what follows from the above.
Results may differ from a plain program's by a relative error of at most 0.00051.
Values may be sent and summed in bfloat16 or wider, within the bound.
A program may use at most 64 MiB of HBM per device.

v0:
```python
import functools

import jax
import jax.numpy as jnp
from jax import lax
from jax.sharding import Mesh
from jax.sharding import PartitionSpec as P

COLS = 1024
HID = 8192
BLOCK = 16
DP = ("dp_0", "dp_1", "dp_2")
DP_SHARD = ("dp_0", "dp_1", "dp_2", "shard_0", "shard_1")
SHARD = ("shard_0", "shard_1")


clip_ratio = 0.25
epsilon = 1e-06


def one_axis_at_a_time(shard, axes):
    return functools.reduce(lax.psum, axes, shard)


def add_sources(received):
    return jnp.sum(received, axis=0, dtype=jnp.float32)


def local(hidden_acts, out_grad, token_ids, trigger, stale, aggregate_prev):
    real_mask = (token_ids[0] != 0).astype(jnp.bfloat16)
    masked = out_grad[0] * real_mask[:, None]
    hidden = hidden_acts[0]
    stale_rows = stale[0]
    row_flags = jnp.repeat(trigger[0], BLOCK).astype(jnp.float32)[:, None]
    owners = lax.axis_size(DP)
    own_rows = aggregate_prev.shape[1]
    width = stale_rows.shape[1]
    local_count = jnp.sum(trigger.astype(jnp.float32))
    triggered = one_axis_at_a_time(local_count, DP_SHARD)
    gradient = lax.dot_general(
        hidden, masked, (((0,), (0,)), ((), ())), preferred_element_type=jnp.float32
    )
    delta = (
        (row_flags * (gradient - stale_rows.astype(jnp.float32)))
        .astype(jnp.bfloat16)
        .reshape(owners, own_rows, width)
    )
    received = lax.all_to_all(delta, DP, split_axis=0, concat_axis=0, tiled=True)
    summed = add_sources(received)
    aggregate = aggregate_prev[0] + summed
    squares = jnp.sum(aggregate * aggregate)
    square_total = one_axis_at_a_time(squares, DP_SHARD)
    limit = clip_ratio * jnp.sqrt(jnp.asarray(HID * COLS, jnp.float32))
    clip_factor = jnp.minimum(1.0, limit / jnp.sqrt(square_total + epsilon))
    return (aggregate[None], (aggregate * clip_factor)[None], triggered)


def solution(mesh):
    finer = Mesh(
        mesh.devices.reshape(4, 2, 16, 2, 2), ("dp_0", "dp_1", "dp_2", "shard_0", "shard_1")
    )
    in_specs = (
        P(DP, None, SHARD),
        P(DP, None, None),
        P(DP, None),
        P(DP, SHARD),
        P(DP, SHARD, None),
        P(SHARD, DP, None),
    )
    out_specs = (P(SHARD, DP, None), P(SHARD, DP, None), P())
    return jax.shard_map(local, mesh=finer, in_specs=in_specs, out_specs=out_specs, check_vma=False)
```

profile of v0, /device:TPU:1, one launch (start us, length us, event | category | flops | bytes accessed | tf_op | source)
XLA Modules:
  0.0 289.7 jit_solution(11659904116884867124)
XLA Ops:
  0.6 0.0 copy-start
  0.6 0.0 copy-start.4
  0.7 0.0 copy-start.3
  0.7 0.0 copy-start.1
  0.7 6.6 %copy.10 = bf16[1,2048,1024]{1,2,0:T(8,128)(2,1)} copy(bf16[1,2048,1024]{2,1,0:T(8,128)(2,1)} %param.10) | data formatting | bytes 8388608 | tf_op args[4]
  7.3 0.0 copy-done.4
  7.3 0.1 broadcast_in_dim.2
  7.4 0.1 convert_element_type.39
  7.4 0.0 copy-done.3
  7.5 0.0 copy-done
  7.5 0.0 copy-done.1
  7.5 5.5 %fusion.1 = bf16[2048,1024]{0,1:T(8,128)(2,1)} fusion(bf16[1,2048,1024]{1,2,0:T(8,128)(2,1)} %copy.10, f32[2048]{0:T(1024)S(1)} %convert_element_type.39, bf16[1,128,2048]{2,1,0:T(8,128)(2,1)S(1)} %copy-done, bf16[1,128,1024]{2,1,0:T(8,128)(2,1)S(1)} %copy-done.1, bf16[128]{0:T(256)(128)(2,1)S(1)} %fusion.8), kind=kOutput, calls=%fused_computation.2 | convolution fusion | flops 545390592 | bytes 9183488 | tf_op jit(solution)/shard_map/dot_general | solution.py:40
  13.0 6.4 %copy.11 = bf16[2048,1024]{1,0:T(8,128)(2,1)} copy(bf16[2048,1024]{0,1:T(8,128)(2,1)} %fusion.1) | data formatting | bytes 8388608 | tf_op jit(solution)/shard_map/convert_element_type | solution.py:45
  19.4 22.0 %all-to-all-start = ((bf16[128,16,1024]{2,1,0:T(8,128)(2,1)}), bf16[128,16,1024]{2,1,0:T(8,128)(2,1)}, u32[]{:S(2)}, u32[]{:S(2)}) async-start(bf16[128,16,1024]{2,1,0:T(8,128)(2,1)} %bitcast.25), calls=%async_computation | async-start | bytes 8388608 | tf_op jit(solution)/shard_map/all_to_all | solution.py:48
  41.4 0.0 copy-start.2
  41.4 0.6 convert_reduce_fusion.1
  42.0 183.0 %all-to-all-done = bf16[128,16,1024]{2,1,0:T(8,128)(2,1)} async-done(((bf16[128,16,1024]{2,1,0:T(8,128)(2,1)}), bf16[128,16,1024]{2,1,0:T(8,128)(2,1)}, u32[]{:S(2)}, u32[]{:S(2)}) %all-to-all-start) | async-done | bytes 4194336 | tf_op jit(solution)/shard_map/all_to_all | solution.py:48
  225.0 2.8 convert_reduce_fusion
  227.8 0.0 copy-done.2
  227.8 0.6 fusion.7
  228.4 7.3 %all-reduce.1 = (f32[]{:T(128)}, f32[]{:T(128)}) all-reduce(f32[]{:T(128)} %fusion.7, f32[]{:T(128)} %convert_reduce_fusion.1), channel_id=1, replica_groups=mesh['dp_0'=4,'dp_1'=2,'dp_2'=16,'shard_0'=2,'shard_1'=2] {'dp_0'}, use_global_device_ids=true, to_apply=%region_2.0 | all-reduce | flops 2 | bytes 16 | tf_op jit(solution)/shard_map/psum | solution.py:22
  235.7 4.4 %all-reduce.4 = (f32[]{:T(128)}, f32[]{:T(128)}) all-reduce(f32[]{:T(128)} %get-tuple-element.5, f32[]{:T(128)} %get-tuple-element.6), channel_id=1, replica_groups=mesh['dp_0'=4,'dp_1'=2,'dp_2'=16,'shard_0'=2,'shard_1'=2] {'dp_1'}, use_global_device_ids=true, to_apply=%region_3.0 | all-reduce | flops 2 | bytes 16 | tf_op jit(solution)/shard_map/psum | solution.py:22
  240.1 28.1 %all-reduce = (f32[]{:T(128)}, f32[]{:T(128)}) all-reduce(f32[]{:T(128)} %get-tuple-element.11, f32[]{:T(128)} %get-tuple-element.12), channel_id=1, replica_groups=mesh['dp_0'=4,'dp_1'=2,'dp_2'=16,'shard_0'=2,'shard_1'=2] {'dp_2'}, use_global_device_ids=true, to_apply=%region_4.0 | all-reduce | flops 2 | bytes 16 | tf_op jit(solution)/shard_map/psum | solution.py:22
  268.2 5.9 %all-reduce.3 = (f32[]{:T(128)}, f32[]{:T(128)}) all-reduce(f32[]{:T(128)} %get-tuple-element.3, f32[]{:T(128)} %get-tuple-element.4), channel_id=1, replica_groups=mesh['dp_0'=4,'dp_1'=2,'dp_2'=16,'shard_0'=2,'shard_1'=2] {'shard_0'}, use_global_device_ids=true, to_apply=%region_5.0 | all-reduce | flops 2 | bytes 16 | tf_op jit(solution)/shard_map/psum | solution.py:22
  274.1 14.2 %all-reduce.2 = (f32[]{:T(128)}, f32[]{:T(128)}) all-reduce(f32[]{:T(128)} %get-tuple-element.9, f32[]{:T(128)} %get-tuple-element.10), channel_id=1, replica_groups=mesh['dp_0'=4,'dp_1'=2,'dp_2'=16,'shard_0'=2,'shard_1'=2] {'shard_1'}, use_global_device_ids=true, to_apply=%region_6.0 | all-reduce | flops 2 | bytes 16 | tf_op jit(solution)/shard_map/psum | solution.py:22
  289.1 0.7 broadcast_multiply_fusion
  (2 shorter events, 0.0 us)
Async XLA Ops:
  0.6 6.8 %copy-start = (bf16[1,128,2048]{2,1,0:T(8,128)(2,1)S(1)}, bf16[1,128,2048]{2,1,0:T(8,128)(2,1)}, u32[]{:S(2)}) copy-start(bf16[1,128,2048]{2,1,0:T(8,128)(2,1)} %param.6) | copy-start | bytes 1572868
  0.6 6.6 %copy-start.4 = (s32[1,128]{1,0:T(1,128)S(1)}, s32[1,128]{1,0:T(1,128)}, u32[]{:S(2)}) copy-start(s32[1,128]{1,0:T(1,128)} %param.9) | copy-start | bytes 1540
  0.7 6.8 %copy-start.3 = (s32[1,128]{1,0:T(1,128)S(1)}, s32[1,128]{1,0:T(1,128)}, u32[]{:S(2)}) copy-start(s32[1,128]{1,0:T(1,128)} %param.8) | copy-start | bytes 1540
  0.7 6.8 %copy-start.1 = (bf16[1,128,1024]{2,1,0:T(8,128)(2,1)S(1)}, bf16[1,128,1024]{2,1,0:T(8,128)(2,1)}, u32[]{:S(2)}) copy-start(bf16[1,128,1024]{2,1,0:T(8,128)(2,1)} %param.7) | copy-start | bytes 786436
  19.4 205.6 %all-to-all-start = ((bf16[128,16,1024]{2,1,0:T(8,128)(2,1)}), bf16[128,16,1024]{2,1,0:T(8,128)(2,1)}, u32[]{:S(2)}, u32[]{:S(2)}) async-start(bf16[128,16,1024]{2,1,0:T(8,128)(2,1)} %bitcast.25), calls=%async_computation | async-start | bytes 8388608 | tf_op jit(solution)/shard_map/all_to_all | solution.py:48
  41.4 186.5 %copy-start.2 = (f32[1,16,1024]{2,1,0:T(8,128)S(1)}, f32[1,16,1024]{2,1,0:T(8,128)}, u32[]{:S(2)}) copy-start(f32[1,16,1024]{2,1,0:T(8,128)} %param.11) | copy-start | bytes 196612
where the time goes:
time: 290 us
  waiting for transfers between devices  183 us (63%)
  blocking collectives  59.9 us (21%)
  starting transfers between devices  22 us (8%)
  local copies, waits for them, and re-layouts  13.2 us (5%)
  matrix products  5.51 us (2%)
  other arithmetic  4.72 us (2%)
    all_to_all x1, waiting for transfers between devices, local(): lax.all_to_all(delta, DP, split_axis=0, concat_axis=0, tiled=True)  183 us
    psum x5, blocking collectives, one_axis_at_a_time(): return functools.reduce(lax.psum, axes, shard)  59.9 us
    all_to_all x1, starting transfers between devices, local(): lax.all_to_all(delta, DP, split_axis=0, concat_axis=0, tiled=True)  22 us
    unnamed x11, local copies, waits for them, and re-layouts  6.62 us
    convert_element_type x1, local copies, waits for them, and re-layouts, local(): delta = (row_flags * (gradient - stale_rows.astype(jnp.float32))).astype(...  6.4 us
  transfers between devices with their start and end apart: 1, of which 1 were waited for; matrix products, arithmetic and copies ran while one was open for 0% of the time, Pallas kernels for 0%

commit v1 on v0

v1 whole, which is shorter than its diff:
```python
import functools

import jax
import jax.numpy as jnp
from jax import lax
from jax.experimental import pallas as pl
from jax.experimental.pallas import tpu as pltpu
from jax.sharding import PartitionSpec as P

BLOCK = 16
NY, NX, NZ = 4, 2, 16
CHUNKS = 4
MESH = pl.DeviceIdType.MESH

clip_ratio = 0.25
epsilon = 1e-06


def reduce_kernel(
    rows, cols,
    hidden_ref, grad_ref, ids_ref, trigger_ref, prev_ref, stale_ref,
    aggregate_ref, sums_ref,
    hidden_t, masked, flags, delta, y_recv, x_data, x_recv, z_data, z_mid, z_recv, squares,
    stale_sem, y_send_sem, y_recv_sem, x_send_sem, x_recv_sem, z_send_sem, z_recv_sem,
):
    tokens = hidden_ref.shape[0]
    width = cols // CHUNKS
    half = rows // (NY * NX)
    own = half // NZ
    me = lax.axis_index("dp")
    y = me // (NX * NZ)
    x = (me // NZ) % NX
    z = me % NZ
    y_right, y_left, y_far = (y + 1) % NY, (y + NY - 1) % NY, (y + 2) % NY

    def at(yy, xx, zz):
        return {"dp": yy * (NX * NZ) + xx * NZ + zz}

    right, left = at(y_right, x, z), at(y_left, x, z)
    across = at(y, 1 - x, z)

    def z_off(k):
        return (z + NZ + k) % NZ

    barrier = pltpu.get_barrier_semaphore()
    peers = [right, left, across] + [at(y, x, z_off(s * k)) for k in range(1, 5) for s in (1, -1)]
    for peer in peers:
        pl.semaphore_signal(barrier, inc=1, device_id=peer, device_id_type=MESH)

    def stale_copy(c):
        return pltpu.make_async_copy(
            stale_ref.at[:, pl.ds(pl.multiple_of(c * width, 128), width)],
            delta.at[c], stale_sem.at[c],
        )

    for c in range(CHUNKS):
        stale_copy(c).start()

    keep = jnp.broadcast_to(ids_ref[...], (tokens, tokens)).T != 0
    keep = jnp.where(keep, 1.0, 0.0)
    for c in range(CHUNKS):
        for j in range(width // 128):
            part = grad_ref[:, c * width + j * 128 : c * width + (j + 1) * 128]
            masked[c, :, j * 128 : (j + 1) * 128] = (part.astype(jnp.float32) * keep).astype(jnp.bfloat16)
    blocks = rows // BLOCK
    sent = jnp.broadcast_to(trigger_ref[...].astype(jnp.float32), (blocks, blocks)).T
    for j in range(width // 128):
        flags[:, j * 128 : (j + 1) * 128] = sent

    @pl.loop(0, rows // 128)
    def _(i):
        start = pl.multiple_of(i * 128, 128)
        hidden_t[pl.ds(start, 128), :] = hidden_ref[:, pl.ds(start, 128)].T

    squares[...] = jnp.zeros_like(squares)

    def rows_of(yy, xx):
        return pl.ds(pl.multiple_of(yy * (NX * half) + xx * half, half), half)

    def y_copy(c, m):
        yy, xx, device = (
            (y_far, 0, left), (y_far, 1, right),
            (y_left, 1, left), (y_right, 0, right),
            (y_left, 0, left), (y_right, 1, right),
        )[m]
        return pltpu.make_async_remote_copy(
            delta.at[c, rows_of(yy, xx)], y_recv.at[c, m], y_send_sem.at[c, m], y_recv_sem.at[c, m],
            device_id=device, device_id_type=MESH,
        )

    def x_copy(c):
        return pltpu.make_async_remote_copy(
            x_data.at[c, 1 - x], x_recv.at[c], x_send_sem.at[c], x_recv_sem.at[c],
            device_id=across, device_id_type=MESH,
        )

    def z_copy(c, m):
        if m < 4:
            source, to = z_data.at[c, z_off(-(m + 5))], -(m + 1)
        elif m < 7:
            source, to = z_data.at[c, z_off(m + 1)], m - 3
        elif m < 9:
            source, to = z_mid.at[c, m - 7], (-4, 4)[m - 7]
        elif m < 12:
            source, to = z_data.at[c, z_off(-(m - 8))], -(m - 8)
        else:
            source, to = z_data.at[c, z_off(m - 11)], m - 11
        return pltpu.make_async_remote_copy(
            source, z_recv.at[c, m], z_send_sem.at[c, m], z_recv_sem.at[c, m],
            device_id=at(y, x, z_off(to)), device_id_type=MESH,
        )

    tile = 256

    def compute(c):
        stale_copy(c).wait()

        @pl.loop(0, rows // tile)
        def _(g):
            start = pl.multiple_of(g * tile, tile)
            gradient = jnp.dot(
                hidden_t[pl.ds(start, tile), :], masked[c], preferred_element_type=jnp.float32
            )
            diff = gradient - delta[c, pl.ds(start, tile), :].astype(jnp.float32)
            for i in range(tile // BLOCK):
                flag = flags[pl.ds(g * (tile // BLOCK) + i, 1), :]
                delta[c, pl.ds(start + i * BLOCK, BLOCK), :] = (
                    flag * diff[i * BLOCK : (i + 1) * BLOCK]
                ).astype(jnp.bfloat16)

    def send_first(c):
        for m in range(4):
            y_copy(c, m).start()

    def pass_on(c):
        for m, yy, xx in ((0, y_left, 0), (1, y_right, 1)):
            y_copy(c, m).wait_recv()
            where = rows_of(yy, xx)
            total = delta[c, where, :].astype(jnp.float32) + y_recv[c, m].astype(jnp.float32)
            delta[c, where, :] = total.astype(jnp.bfloat16)
            y_copy(c, m + 4).start()

    def sum_y(c):
        for m in (2, 3, 4, 5):
            y_copy(c, m).wait_recv()
        for xx, first, second in ((0, 3, 4), (1, 2, 5)):
            x_data[c, xx] = (
                delta[c, rows_of(y, xx), :].astype(jnp.float32)
                + y_recv[c, first].astype(jnp.float32)
                + y_recv[c, second].astype(jnp.float32)
            )
        x_copy(c).start()

    def sum_x(c):
        x_copy(c).wait_recv()
        for k in range(NZ):
            part = pl.ds(k * own, own)
            z_data[c, k] = x_data[c, x, part, :] + x_recv[c, part, :]
        for m in (3, 2, 1, 0, 6, 5, 4, 9, 10, 11, 12, 13, 14):
            z_copy(c, m).start()

    def pass_on_z(c):
        for m in range(7):
            z_copy(c, m).wait_recv()
        low = z_data[c, z_off(-4)] + z_recv[c, 0] + z_recv[c, 1]
        z_mid[c, 0] = low + z_recv[c, 2] + z_recv[c, 3]
        z_copy(c, 7).start()
        z_mid[c, 1] = z_data[c, z_off(4)] + z_recv[c, 4] + z_recv[c, 5] + z_recv[c, 6]
        z_copy(c, 8).start()

    def finish(c):
        for m in range(7, 15):
            z_copy(c, m).wait_recv()
        total = z_data[c, z]
        for m in range(7, 15):
            total = total + z_recv[c, m]
        where = pl.ds(pl.multiple_of(c * width, 128), width)
        total = prev_ref[:, where] + total
        aggregate_ref[:, where] = total
        squares[...] += total * total

    compute(0)
    pl.semaphore_wait(barrier, len(peers))

    @pl.loop(0, CHUNKS + 5)
    def _(s):
        @pl.when(s < CHUNKS)
        def _():
            @pl.when(s > 0)
            def _():
                compute(s)

            send_first(s)

        for lag, stage in enumerate((pass_on, sum_y, sum_x, pass_on_z, finish), 1):

            @pl.when((s >= lag) & (s < CHUNKS + lag))
            def _(lag=lag, stage=stage):
                stage(s - lag)

    sums_ref[0] = jnp.sum(squares[...])
    sums_ref[1] = jnp.sum(trigger_ref[...].astype(jnp.float32))

    @pl.loop(0, CHUNKS)
    def _(c):
        for m in range(6):
            y_copy(c, m).wait_send()
        x_copy(c).wait_send()
        for m in range(15):
            z_copy(c, m).wait_send()


def local(hidden_acts, out_grad, token_ids, trigger, stale, aggregate_prev):
    tokens, rows = hidden_acts.shape[1:]
    cols = out_grad.shape[2]
    width = cols // CHUNKS
    half = rows // (NY * NX)
    own = aggregate_prev.shape[1]
    vmem = pl.BlockSpec(memory_space=pltpu.VMEM)
    aggregate, sums = pl.pallas_call(
        functools.partial(reduce_kernel, rows, cols),
        out_shape=(
            jax.ShapeDtypeStruct((own, cols), jnp.float32),
            jax.ShapeDtypeStruct((2,), jnp.float32),
        ),
        in_specs=[vmem] * 5 + [pl.BlockSpec(memory_space=pl.ANY)],
        out_specs=(vmem, pl.BlockSpec(memory_space=pltpu.SMEM)),
        scratch_shapes=[
            pltpu.VMEM((rows, tokens), jnp.bfloat16),
            pltpu.VMEM((CHUNKS, tokens, width), jnp.bfloat16),
            pltpu.VMEM((rows // BLOCK, width), jnp.float32),
            pltpu.VMEM((CHUNKS, rows, width), jnp.bfloat16),
            pltpu.VMEM((CHUNKS, 6, half, width), jnp.bfloat16),
            pltpu.VMEM((CHUNKS, NX, half, width), jnp.float32),
            pltpu.VMEM((CHUNKS, half, width), jnp.float32),
            pltpu.VMEM((CHUNKS, NZ, own, width), jnp.float32),
            pltpu.VMEM((CHUNKS, 2, own, width), jnp.float32),
            pltpu.VMEM((CHUNKS, 15, own, width), jnp.float32),
            pltpu.VMEM((own, width), jnp.float32),
            pltpu.SemaphoreType.DMA((CHUNKS,)),
            pltpu.SemaphoreType.DMA((CHUNKS, 6)),
            pltpu.SemaphoreType.DMA((CHUNKS, 6)),
            pltpu.SemaphoreType.DMA((CHUNKS,)),
            pltpu.SemaphoreType.DMA((CHUNKS,)),
            pltpu.SemaphoreType.DMA((CHUNKS, 15)),
            pltpu.SemaphoreType.DMA((CHUNKS, 15)),
        ],
        compiler_params=pltpu.CompilerParams(
            collective_id=0, has_side_effects=True, vmem_limit_bytes=48 * 1024 * 1024
        ),
        name="reduce_deltas",
    )(hidden_acts[0], out_grad[0], token_ids, trigger, aggregate_prev[0], stale[0])
    square_total, triggered = lax.psum((sums[0], sums[1]), ("dp", "shard"))
    limit = clip_ratio * jnp.sqrt(jnp.asarray(4 * rows * cols, jnp.float32))
    clip_factor = jnp.minimum(1.0, limit / jnp.sqrt(square_total + epsilon))
    return (aggregate[None], (aggregate * clip_factor)[None], triggered)


def solution(mesh):
    in_specs = (
        P("dp", None, "shard"),
        P("dp", None, None),
        P("dp", None),
        P("dp", "shard"),
        P("dp", "shard", None),
        P("shard", "dp", None),
    )
    out_specs = (P("shard", "dp", None), P("shard", "dp", None), P())
    return jax.shard_map(local, mesh=mesh, in_specs=in_specs, out_specs=out_specs, check_vma=False)
```

time: 290 us -> 187 us (0.64)
  waiting for transfers between devices: 183 us -> 0 us
  Pallas kernels: 0 us -> 72.3 us
  blocking collectives: 59.9 us -> 105 us
  starting transfers between devices: 22 us -> 0 us
  local copies, waits for them, and re-layouts: 13.2 us -> 7.53 us
  matrix products: 5.51 us -> 0 us
  other arithmetic: 4.72 us -> 0.64 us
    all_to_all x1 -> x0, waiting for transfers between devices: 183 us -> none  [local(): lax.all_to_all(delta, DP, split_axis=0, concat_axis=0, tiled=True)]
    pallas_call x0 -> x1, Pallas kernels: none -> 72.3 us  [local(): pl.pallas_call(functools.partial(reduce_kernel, rows, cols), out_shape=(j...]
    psum x5 -> x1, blocking collectives: 59.9 us -> 105 us  [local(): square_total, triggered = lax.psum((sums[0], sums[1]), ('dp', 'shard'))]
    all_to_all x1 -> x0, starting transfers between devices: 22 us -> none  [local(): lax.all_to_all(delta, DP, split_axis=0, concat_axis=0, tiled=True)]
    convert_element_type x2 -> x0, local copies, waits for them, and re-layouts: 6.49 us -> none  [the longest x1 6.4 us: local(): delta = (row_flags * (gradient - stale_rows.astype(jnp.float32))).astype(...]
    dot_general x1 -> x0, matrix products: 5.51 us -> none  [local(): lax.dot_general(hidden, masked, (((0,), (0,)), ((), ())), preferred_eleme...]
    reduce_sum x3 -> x0, other arithmetic: 4.05 us -> none  [the longest x1 2.83 us: add_sources(): return jnp.sum(received, axis=0, dtype=jnp.float32)]
    unnamed x11 -> x13, local copies, waits for them, and re-layouts: 6.62 us -> 6.95 us
  transfers between devices with their start and end apart: 1 -> 0, of which waited for: 1 -> 0; matrix products, arithmetic and copies ran while one was open for 0% -> 0% of each run, Pallas kernels for 0% -> 0%
where the time goes in v1:
time: 187 us
  blocking collectives  105 us (56%)
  Pallas kernels  72.3 us (39%)
  local copies, waits for them, and re-layouts  7.53 us (4%)
    psum x1, blocking collectives, local(): square_total, triggered = lax.psum((sums[0], sums[1]), ('dp', 'shard'))  105 us
    pallas_call x1, Pallas kernels, local(): pl.pallas_call(functools.partial(reduce_kernel, rows, cols), out_shape=(j...  72.3 us
    unnamed x13, local copies, waits for them, and re-layouts  6.95 us

profile of v1, /device:TPU:1, one launch (start us, length us, event | category | flops | bytes accessed | tf_op | source)
XLA Modules:
  0.0 186.5 jit_solution(4770568752291975561)
XLA Ops:
  0.6 0.0 copy-start
  0.6 2.2 %copy-done = bf16[1,2048,1024]{2,1,0:T(8,128)(2,1)S(1)} copy-done((bf16[1,2048,1024]{2,1,0:T(8,128)(2,1)S(1)}, bf16[1,2048,1024]{2,1,0:T(8,128)(2,1)}, u32[]{:S(2)}) %copy-start) | copy-done | bytes 4194328
  2.8 0.0 copy-start.1
  2.8 1.0 copy-done.1
  3.9 0.0 copy-start.2
  3.9 0.9 copy-done.2
  4.8 0.0 copy-start.3
  4.8 0.8 copy-done.3
  5.7 0.0 copy-start.4
  5.7 0.7 copy-done.4
  6.3 0.0 copy-start.5
  6.3 0.7 copy-done.5
  7.0 72.3 %reduce_deltas.1 = (f32[16,1024]{1,0:T(8,128)S(1)}, f32[2]{0:T(128)S(1)}) custom-call(bf16[128,2048]{1,0:T(8,128)(2,1)S(1)} %bitcast.10, bf16[128,1024]{1,0:T(8,128)(2,1)S(1)} %bitcast.11, s32[1,128]{1,0:T(1,128)S(1)} %copy-done.4, s32[1,128]{1,0:T(1,128)S(1)} %copy-done.5, f32[16,1024]{1,0:T(8,128)S(1)} %bitcast.13, bf16[2048,1024]{1,0:T(8,128)(2,1)S(1)} %bitcast.9), custom_call_target="tpu_custom_call" | custom-call | tf_op jit(solution)/shard_map/reduce_deltas/pallas_call | solution.py:220
  79.3 0.6 fusion
  79.8 104.7 %all-reduce = (f32[]{:T(128)}, f32[]{:T(128)}) all-reduce(f32[]{:T(128)} %bitcast.5, f32[]{:T(128)} %bitcast.7), channel_id=1, replica_groups=mesh['dp'=128,'shard'=4] {'dp','shard'}, use_global_device_ids=true, to_apply=%region_0.0 | all-reduce | flops 2 | bytes 16 | tf_op jit(solution)/shard_map/psum | solution.py:253
  185.3 0.6 multiply_bitcast_fusion
  185.9 0.6 copy.10
Async XLA Ops:
  0.6 2.2 %copy-start = (bf16[1,2048,1024]{2,1,0:T(8,128)(2,1)S(1)}, bf16[1,2048,1024]{2,1,0:T(8,128)(2,1)}, u32[]{:S(2)}) copy-start(bf16[1,2048,1024]{2,1,0:T(8,128)(2,1)} %param.10) | copy-start | bytes 12582916
  2.8 1.0 copy-start.1
  3.9 0.9 copy-start.2
  4.8 0.8 copy-start.3
  5.7 0.7 copy-start.4
  6.3 0.7 copy-start.5

commit v2 on v1

v2 whole, which is shorter than its diff:
```python
import functools

import jax
import jax.numpy as jnp
from jax import lax
from jax.experimental import pallas as pl
from jax.experimental.pallas import tpu as pltpu
from jax.sharding import PartitionSpec as P

BLOCK = 16
NY, NX, NZ = 4, 2, 16
NG = 2 * NX
CHUNKS = 8
MESH = pl.DeviceIdType.MESH

clip_ratio = 0.25
epsilon = 1e-06


def reduce_kernel(
    rows, cols,
    ids_hbm, trigger_hbm, grad_hbm, hidden_hbm, prev_hbm, stale_hbm,
    total_ref, factor_ref, count_ref,
    ids_ref, trigger_ref, grad_ref, hidden_ref, prev_ref,
    hidden_t, masked, keep, flags, delta, y_recv, x_data, x_recv, z_data, z_mid, z_recv, squares,
    n_data, n_recv_z, n_recv_p,
    input_sem, stale_sem, y_send_sem, y_recv_sem, x_send_sem, x_recv_sem, z_send_sem, z_recv_sem,
    n_send_sem, n_recv_sem,
):
    tokens = hidden_ref.shape[0]
    width = cols // CHUNKS
    half = rows // (NY * NX)
    own = half // NZ
    me = lax.axis_index("dp")
    shard = lax.axis_index("shard")
    y = me // (NX * NZ)
    x = (me // NZ) % NX
    z = me % NZ
    core = shard % 2
    group_x = (shard // 2) * NX + x
    y_right, y_left, y_far = (y + 1) % NY, (y + NY - 1) % NY, (y + 2) % NY

    def at(yy, xx, zz):
        return {"dp": yy * (NX * NZ) + xx * NZ + zz}

    right, left = at(y_right, x, z), at(y_left, x, z)
    across = at(y, 1 - x, z)

    def z_off(k):
        return (z + NZ + k) % NZ

    plane = [(oy, ox, oc) for oy in range(NY) for ox in range(NG) for oc in range(2)][1:]

    far_first = sorted(
        range(len(plane)), key=lambda i: -(min(plane[i][0], NY - plane[i][0]) + min(plane[i][1], NG - plane[i][1]))
    )

    def plane_peer(oy, ox, oc):
        yy, xx, cc = (y + oy) % NY, (group_x + ox) % NG, (core + oc) % 2
        return {"dp": yy * (NX * NZ) + (xx % NX) * NZ + z, "shard": (xx // NX) * 2 + cc}

    inputs = [
        pltpu.make_async_copy(source, target, input_sem.at[i])
        for i, (source, target) in enumerate((
            (ids_hbm, ids_ref), (trigger_hbm, trigger_ref), (grad_hbm, grad_ref),
            (hidden_hbm, hidden_ref), (prev_hbm, prev_ref),
        ))
    ]

    def stale_copy(c):
        return pltpu.make_async_copy(
            stale_hbm.at[:, pl.ds(pl.multiple_of(c * width, 128), width)],
            delta.at[c], stale_sem.at[c],
        )

    for copy in inputs[:4]:
        copy.start()
    for c in range(CHUNKS):
        stale_copy(c).start()
    inputs[4].start()

    barrier = pltpu.get_barrier_semaphore()
    for k in range(1, NZ):
        pl.semaphore_signal(barrier, inc=1, device_id=at(y, x, z_off(k)), device_id_type=MESH)
    for offset in plane:
        pl.semaphore_signal(barrier, inc=1, device_id=plane_peer(*offset), device_id_type=MESH)

    inputs[0].wait()
    inputs[1].wait()
    real = jnp.broadcast_to(ids_ref[...], (tokens, tokens)).T != 0
    real = jnp.where(real, 1.0, 0.0)
    blocks = rows // BLOCK
    sent = jnp.broadcast_to(trigger_ref[...].astype(jnp.float32), (blocks, blocks)).T
    for j in range(width // 128):
        keep[:, j * 128 : (j + 1) * 128] = real
        flags[:, j * 128 : (j + 1) * 128] = sent
    squares[...] = jnp.zeros_like(squares)

    def first_row(yy, xx):
        return pl.multiple_of(yy * (NX * half) + xx * half, half)

    def rows_of(yy, xx):
        return pl.ds(first_row(yy, xx), half)

    def y_copy(c, m):
        yy, xx, device = (
            (y_far, 0, left), (y_far, 1, right),
            (y_left, 1, left), (y_right, 0, right),
            (y_left, 0, left), (y_right, 1, right),
        )[m]
        return pltpu.make_async_remote_copy(
            delta.at[c, rows_of(yy, xx)], y_recv.at[c, m], y_send_sem.at[0], y_recv_sem.at[c, min(m, 2)],
            device_id=device, device_id_type=MESH,
        )

    def x_copy(c):
        return pltpu.make_async_remote_copy(
            x_data.at[c, 1 - x], x_recv.at[c], x_send_sem.at[0], x_recv_sem.at[c],
            device_id=across, device_id_type=MESH,
        )

    def z_copy(c, m):
        if m < 4:
            source, to = z_data.at[c, z_off(-(m + 5))], -(m + 1)
        elif m < 7:
            source, to = z_data.at[c, z_off(m + 1)], m - 3
        elif m < 9:
            source, to = z_mid.at[c, m - 7], (-4, 4)[m - 7]
        elif m < 12:
            source, to = z_data.at[c, z_off(-(m - 8))], -(m - 8)
        else:
            source, to = z_data.at[c, z_off(m - 11)], m - 11
        return pltpu.make_async_remote_copy(
            source, z_recv.at[c, m], z_send_sem.at[0], z_recv_sem.at[c, 0 if m < 7 else 1],
            device_id=at(y, x, z_off(to)), device_id_type=MESH,
        )

    def arrived(ref, sem):
        pltpu.make_async_copy(ref, ref, sem).wait()

    def compute(c, yy, xx, first):
        start = first_row(yy, xx)
        if first:
            for j in range(half // 128):
                part = pl.ds(pl.multiple_of(start + j * 128, 128), 128)
                hidden_t[part, :] = hidden_ref[:, part].T
        gradient = jnp.dot(
            hidden_t[pl.ds(start, half), :], masked[...], preferred_element_type=jnp.float32
        )
        diff = gradient - delta[c, pl.ds(start, half), :].astype(jnp.float32)
        for i in range(half // BLOCK):
            flag = flags[pl.ds(start // BLOCK + i, 1), :]
            delta[c, pl.ds(start + i * BLOCK, BLOCK), :] = (
                flag * diff[i * BLOCK : (i + 1) * BLOCK]
            ).astype(jnp.bfloat16)

    def begin(c, first=False):
        part = grad_ref[:, pl.ds(pl.multiple_of(c * width, 128), width)]
        masked[...] = (part.astype(jnp.float32) * keep[...]).astype(jnp.bfloat16)
        stale_copy(c).wait()
        compute(c, y_far, 0, first)
        compute(c, y_far, 1, first)
        if first:
            pl.semaphore_wait(barrier, NZ - 1 + len(plane))
        y_copy(c, 0).start()
        compute(c, y_left, 1, first)
        y_copy(c, 1).start()
        compute(c, y_right, 0, first)
        y_copy(c, 2).start()
        compute(c, y_left, 0, first)
        y_copy(c, 3).start()
        compute(c, y_right, 1, first)
        compute(c, y, 0, first)
        compute(c, y, 1, first)

    def pass_on(c):
        for m, yy, xx in ((0, y_left, 0), (1, y_right, 1)):
            y_copy(c, m).wait_recv()
            where = rows_of(yy, xx)
            total = delta[c, where, :].astype(jnp.float32) + y_recv[c, m].astype(jnp.float32)
            delta[c, where, :] = total.astype(jnp.bfloat16)
            y_copy(c, m + 4).start()

    def sum_y(c):
        arrived(y_recv.at[c, pl.ds(2, 4)], y_recv_sem.at[c, 2])
        for xx, first, second in ((0, 3, 4), (1, 2, 5)):
            x_data[c, xx] = (
                delta[c, rows_of(y, xx), :].astype(jnp.float32)
                + y_recv[c, first].astype(jnp.float32)
                + y_recv[c, second].astype(jnp.float32)
            )
        x_copy(c).start()

    def sum_x(c):
        x_copy(c).wait_recv()
        for k in range(NZ):
            part = pl.ds(k * own, own)
            z_data[c, k] = x_data[c, x, part, :] + x_recv[c, part, :]
        for m in (3, 2, 1, 0, 6, 5, 4, 11, 10, 9, 14, 13, 12):
            z_copy(c, m).start()

    def pass_on_z(c):
        arrived(z_recv.at[c, pl.ds(0, 7)], z_recv_sem.at[c, 0])
        low = z_data[c, z_off(-4)] + z_recv[c, 0] + z_recv[c, 1]
        z_mid[c, 0] = low + z_recv[c, 2] + z_recv[c, 3]
        z_copy(c, 7).start()
        z_mid[c, 1] = z_data[c, z_off(4)] + z_recv[c, 4] + z_recv[c, 5] + z_recv[c, 6]
        z_copy(c, 8).start()

    def finish(c):
        arrived(z_recv.at[c, pl.ds(7, 8)], z_recv_sem.at[c, 1])
        total = z_data[c, z]
        for m in range(7, 15):
            total = total + z_recv[c, m]
        where = pl.ds(pl.multiple_of(c * width, 128), width)
        total_ref[:, where] = total
        total = prev_ref[:, where] + total
        squares[...] += total * total

    inputs[2].wait()
    inputs[3].wait()
    begin(0, first=True)

    @pl.loop(1, CHUNKS + 5)
    def _(s):
        @pl.when(s < CHUNKS)
        def _():
            begin(s)

        @pl.when(s == 1)
        def _():
            inputs[4].wait()

        for lag, stage in enumerate((pass_on, sum_y, sum_x, pass_on_z, finish), 1):

            @pl.when((s >= lag) & (s < CHUNKS + lag))
            def _(lag=lag, stage=stage):
                stage(s - lag)

    lanes = squares[0:8, 0:128]
    for i in range(own // 8):
        for j in range(width // 128):
            if i + j > 0:
                lanes = lanes + squares[i * 8 : (i + 1) * 8, j * 128 : (j + 1) * 128]
    lanes = jnp.sum(lanes, axis=0, keepdims=True)
    n_data[0, 0:1, :] = lanes
    n_data[0, 1:2, :] = trigger_ref[...].astype(jnp.float32)

    def n_copy(k):
        return pltpu.make_async_remote_copy(
            n_data.at[0], n_recv_z.at[k - 1], n_send_sem.at[0], n_recv_sem.at[0],
            device_id=at(y, x, z_off(k)), device_id_type=MESH,
        )

    def p_copy(i):
        return pltpu.make_async_remote_copy(
            n_data.at[1], n_recv_p.at[i], n_send_sem.at[1], n_recv_sem.at[1],
            device_id=plane_peer(*plane[i]), device_id_type=MESH,
        )

    for k in (8, 7, 9, 6, 10, 5, 11, 4, 12, 3, 13, 2, 14, 1, 15):
        n_copy(k).start()
    arrived(y_recv, y_send_sem.at[0])
    arrived(x_recv, x_send_sem.at[0])
    arrived(z_recv, z_send_sem.at[0])
    arrived(n_recv_z, n_recv_sem.at[0])
    n_data[1] = n_data[0] + jnp.sum(n_recv_z[...], axis=0)
    for i in far_first:
        p_copy(i).start()
    arrived(n_recv_z, n_send_sem.at[0])
    arrived(n_recv_p, n_recv_sem.at[1])
    both = n_data[1] + jnp.sum(n_recv_p[...], axis=0)
    square_total = jnp.sum(both[0:1, :], axis=1, keepdims=True)
    limit = clip_ratio * jnp.sqrt(jnp.full((1, 1), 4 * rows * cols, jnp.float32))
    factor_ref[...] = jnp.minimum(1.0, limit / jnp.sqrt(square_total + epsilon))
    count_ref[...] = jnp.sum(both[1:2, :], axis=1, keepdims=True)

    arrived(n_recv_p, n_send_sem.at[1])


def local(hidden_acts, out_grad, token_ids, trigger, stale, aggregate_prev):
    tokens, rows = hidden_acts.shape[1:]
    cols = out_grad.shape[2]
    width = cols // CHUNKS
    half = rows // (NY * NX)
    own = aggregate_prev.shape[1]
    vmem = pl.BlockSpec(memory_space=pltpu.VMEM)
    hbm = pl.BlockSpec(memory_space=pltpu.HBM)
    bf16, f32 = jnp.bfloat16, jnp.float32
    dma = pltpu.SemaphoreType.DMA
    total, factor, count = pl.pallas_call(
        functools.partial(reduce_kernel, rows, cols),
        out_shape=(
            jax.ShapeDtypeStruct((own, cols), f32),
            jax.ShapeDtypeStruct((1, 1), f32),
            jax.ShapeDtypeStruct((1, 1), f32),
        ),
        in_specs=[hbm] * 6,
        out_specs=(vmem,) * 3,
        scratch_shapes=[
            pltpu.VMEM(token_ids.shape, jnp.int32),
            pltpu.VMEM(trigger.shape, jnp.int32),
            pltpu.VMEM((tokens, cols), bf16),
            pltpu.VMEM((tokens, rows), bf16),
            pltpu.VMEM((own, cols), f32),
            pltpu.VMEM((rows, tokens), bf16),
            pltpu.VMEM((tokens, width), bf16),
            pltpu.VMEM((tokens, width), f32),
            pltpu.VMEM((rows // BLOCK, width), f32),
            pltpu.VMEM((CHUNKS, rows, width), bf16),
            pltpu.VMEM((CHUNKS, 6, half, width), bf16),
            pltpu.VMEM((CHUNKS, NX, half, width), f32),
            pltpu.VMEM((CHUNKS, half, width), f32),
            pltpu.VMEM((CHUNKS, NZ, own, width), f32),
            pltpu.VMEM((CHUNKS, 2, own, width), f32),
            pltpu.VMEM((CHUNKS, 15, own, width), f32),
            pltpu.VMEM((own, width), f32),
            pltpu.VMEM((2, 2, 128), f32),
            pltpu.VMEM((NZ - 1, 2, 128), f32),
            pltpu.VMEM((NY * NG * 2 - 1, 2, 128), f32),
            dma((5,)),
            dma((CHUNKS,)),
            dma((1,)),
            dma((CHUNKS, 3)),
            dma((1,)),
            dma((CHUNKS,)),
            dma((1,)),
            dma((CHUNKS, 2)),
            dma((2,)),
            dma((2,)),
        ],
        compiler_params=pltpu.CompilerParams(
            collective_id=0, has_side_effects=True, vmem_limit_bytes=67_000_000
        ),
        name="reduce_deltas",
    )(token_ids, trigger, out_grad[0], hidden_acts[0], aggregate_prev[0], stale[0])
    aggregate = aggregate_prev[0] + total
    return (aggregate[None], (aggregate * factor)[None], count[0, 0])


def solution(mesh):
    in_specs = (
        P("dp", None, "shard"),
        P("dp", None, None),
        P("dp", None),
        P("dp", "shard"),
        P("dp", "shard", None),
        P("shard", "dp", None),
    )
    out_specs = (P("shard", "dp", None), P("shard", "dp", None), P())
    return jax.shard_map(local, mesh=mesh, in_specs=in_specs, out_specs=out_specs, check_vma=False)
```

time: 187 us -> 90.4 us (0.48)
  blocking collectives: 105 us -> 0 us
  Pallas kernels: 72.3 us -> 85.6 us
  local copies, waits for them, and re-layouts: 7.53 us -> 0 us
    psum x1 -> x0, blocking collectives: 105 us -> none  [local(): square_total, triggered = lax.psum((sums[0], sums[1]), ('dp', 'shard'))]
    pallas_call x1, Pallas kernels: 72.3 us -> 85.6 us  [local(): pl.pallas_call(functools.partial(reduce_kernel, rows, cols), out_shape=(j...]
    unnamed x13 -> x0, local copies, waits for them, and re-layouts: 6.95 us -> none
where the time goes in v2:
time: 90.4 us; the launch traced here: 90.2 us
  Pallas kernels  85.6 us (95%)
  between operations  2.46 us (3%)
  other arithmetic  2.09 us (2%)
    pallas_call x1, Pallas kernels, local(): pl.pallas_call(functools.partial(reduce_kernel, rows, cols), out_shape=(j...  85.6 us
    broadcast_in_dim x1, other arithmetic, local(): return (aggregate[None], (aggregate * factor)[None], count[0, 0])  2.09 us

profile of v2, /device:TPU:1, one launch (start us, length us, event | category | flops | bytes accessed | tf_op | source)
XLA Modules:
  0.0 90.2 jit_solution(5060350052790269780)
XLA Ops:
  0.6 85.6 %reduce_deltas.1 = (f32[16,1024]{1,0:T(8,128)}, f32[1,1]{1,0:T(1,128)}, f32[1,1]{1,0:T(1,128)}) custom-call(s32[1,128]{1,0:T(1,128)} %ids_hbm.1, s32[1,128]{1,0:T(1,128)} %trigger_hbm.1, bf16[128,1024]{1,0:T(8,128)(2,1)} %bitcast.15, bf16[128,2048]{1,0:T(8,128)(2,1)} %bitcast.13, f32[16,1024]{1,0:T(8,128)} %bitcast.14, bf16[2048,1024]{1,0:T(8,128)(2,1)} %bitcast.12), custom_call_target="tpu_custom_call" | custom-call | tf_op jit(solution)/shard_map/reduce_deltas/pallas_call | solution.py:291
  86.3 2.1 %multiply_bitcast_fusion = (f32[1,16,1024]{2,1,0:T(8,128)}, f32[1,16,1024]{2,1,0:T(8,128)}) fusion(f32[]{:T(128)} %bitcast.5, f32[16,1024]{1,0:T(8,128)} %get-tuple-element.6, f32[1,16,1024]{2,1,0:T(8,128)} %param.11), kind=kLoop, calls=%fused_computation | loop fusion | flops 32768 | bytes 262148 | tf_op jit(solution)/shard_map/broadcast_in_dim | solution.py:338

commit v3 on v2

--- a/solution.py
+++ b/solution.py
@@ -20,12 +20,12 @@
 def reduce_kernel(
     rows, cols,
     ids_hbm, trigger_hbm, grad_hbm, hidden_hbm, prev_hbm, stale_hbm,
-    total_ref, factor_ref, count_ref,
+    total_hbm, factor_ref, count_ref,
     ids_ref, trigger_ref, grad_ref, hidden_ref, prev_ref,
-    hidden_t, masked, keep, flags, delta, y_recv, x_data, x_recv, z_data, z_mid, z_recv, squares,
+    total_ref, hidden_t, masked, keep, flags, delta, y_recv, x_data, x_recv, z_data, z_mid, z_recv, squares,
     n_data, n_recv_z, n_recv_p,
     input_sem, stale_sem, y_send_sem, y_recv_sem, x_send_sem, x_recv_sem, z_send_sem, z_recv_sem,
-    n_send_sem, n_recv_sem,
+    n_send_sem, n_recv_sem, word_sem,
 ):
     tokens = hidden_ref.shape[0]
     width = cols // CHUNKS
@@ -59,11 +59,11 @@
         yy, xx, cc = (y + oy) % NY, (group_x + ox) % NG, (core + oc) % 2
         return {"dp": yy * (NX * NZ) + (xx % NX) * NZ + z, "shard": (xx // NX) * 2 + cc}
 
-    inputs = [
+    moves = [
         pltpu.make_async_copy(source, target, input_sem.at[i])
         for i, (source, target) in enumerate((
             (ids_hbm, ids_ref), (trigger_hbm, trigger_ref), (grad_hbm, grad_ref),
-            (hidden_hbm, hidden_ref), (prev_hbm, prev_ref),
+            (hidden_hbm, hidden_ref), (prev_hbm, prev_ref), (total_ref, total_hbm),
         ))
     ]
 
@@ -73,20 +73,23 @@
             delta.at[c], stale_sem.at[c],
         )
 
-    for copy in inputs[:4]:
+    for copy in moves[:4]:
         copy.start()
-    for c in range(CHUNKS):
-        stale_copy(c).start()
-    inputs[4].start()
+    stale_copy(0).start()
+    stale_copy(1).start()
 
     barrier = pltpu.get_barrier_semaphore()
-    for k in range(1, NZ):
-        pl.semaphore_signal(barrier, inc=1, device_id=at(y, x, z_off(k)), device_id_type=MESH)
-    for offset in plane:
-        pl.semaphore_signal(barrier, inc=1, device_id=plane_peer(*offset), device_id_type=MESH)
-
-    inputs[0].wait()
-    inputs[1].wait()
+    near = [right, left, across, at(y, x, z_off(1)), at(y, x, z_off(-1))]
+    near += [plane_peer(0, 0, 1), plane_peer(0, NX, 0), plane_peer(0, NX, 1)]
+    for peer in near:
+        pl.semaphore_signal(barrier, inc=1, device_id=peer, device_id_type=MESH)
+
+    def tell_z(i):
+        for k in (1, -1):
+            pl.semaphore_signal(word_sem.at[i], inc=1, device_id=at(y, x, z_off(k)), device_id_type=MESH)
+
+    moves[0].wait()
+    moves[1].wait()
     real = jnp.broadcast_to(ids_ref[...], (tokens, tokens)).T != 0
     real = jnp.where(real, 1.0, 0.0)
     blocks = rows // BLOCK
@@ -158,10 +161,16 @@
         part = grad_ref[:, pl.ds(pl.multiple_of(c * width, 128), width)]
         masked[...] = (part.astype(jnp.float32) * keep[...]).astype(jnp.bfloat16)
         stale_copy(c).wait()
+
+        @pl.when(c + 2 < CHUNKS)
+        def _():
+            stale_copy(c + 2).start()
+
         compute(c, y_far, 0, first)
         compute(c, y_far, 1, first)
         if first:
-            pl.semaphore_wait(barrier, NZ - 1 + len(plane))
+            pl.semaphore_wait(barrier, len(near))
+            tell_z(0)
         y_copy(c, 0).start()
         compute(c, y_left, 1, first)
         y_copy(c, 1).start()
@@ -217,9 +226,10 @@
         total = prev_ref[:, where] + total
         squares[...] += total * total
 
-    inputs[2].wait()
-    inputs[3].wait()
+    moves[2].wait()
+    moves[3].wait()
     begin(0, first=True)
+    moves[4].start()
 
     @pl.loop(1, CHUNKS + 5)
     def _(s):
@@ -227,9 +237,15 @@
         def _():
             begin(s)
 
-        @pl.when(s == 1)
-        def _():
-            inputs[4].wait()
+        for i in range(3):
+
+            @pl.when(s == i + 1)
+            def _(i=i):
+                pl.semaphore_wait(word_sem.at[i], 2)
+                if i < 2:
+                    tell_z(i + 1)
+                else:
+                    moves[4].wait()
 
         for lag, stage in enumerate((pass_on, sum_y, sum_x, pass_on_z, finish), 1):
 
@@ -260,6 +276,7 @@
 
     for k in (8, 7, 9, 6, 10, 5, 11, 4, 12, 3, 13, 2, 14, 1, 15):
         n_copy(k).start()
+    moves[5].start()
     arrived(y_recv, y_send_sem.at[0])
     arrived(x_recv, x_send_sem.at[0])
     arrived(z_recv, z_send_sem.at[0])
@@ -268,6 +285,7 @@
     for i in far_first:
         p_copy(i).start()
     arrived(n_recv_z, n_send_sem.at[0])
+    moves[5].wait()
     arrived(n_recv_p, n_recv_sem.at[1])
     both = n_data[1] + jnp.sum(n_recv_p[...], axis=0)
     square_total = jnp.sum(both[0:1, :], axis=1, keepdims=True)
@@ -296,12 +314,13 @@
             jax.ShapeDtypeStruct((1, 1), f32),
         ),
         in_specs=[hbm] * 6,
-        out_specs=(vmem,) * 3,
+        out_specs=(hbm, vmem, vmem),
         scratch_shapes=[
             pltpu.VMEM(token_ids.shape, jnp.int32),
             pltpu.VMEM(trigger.shape, jnp.int32),
             pltpu.VMEM((tokens, cols), bf16),
             pltpu.VMEM((tokens, rows), bf16),
+            pltpu.VMEM((own, cols), f32),
             pltpu.VMEM((own, cols), f32),
             pltpu.VMEM((rows, tokens), bf16),
             pltpu.VMEM((tokens, width), bf16),
@@ -318,7 +337,7 @@
             pltpu.VMEM((2, 2, 128), f32),
             pltpu.VMEM((NZ - 1, 2, 128), f32),
             pltpu.VMEM((NY * NG * 2 - 1, 2, 128), f32),
-            dma((5,)),
+            dma((6,)),
             dma((CHUNKS,)),
             dma((1,)),
             dma((CHUNKS, 3)),
@@ -328,9 +347,10 @@
             dma((CHUNKS, 2)),
             dma((2,)),
             dma((2,)),
+            pltpu.SemaphoreType.REGULAR((3,)),
         ],
         compiler_params=pltpu.CompilerParams(
-            collective_id=0, has_side_effects=True, vmem_limit_bytes=67_000_000
+            collective_id=0, has_side_effects=True, vmem_limit_bytes=66_900_000
         ),
         name="reduce_deltas",
     )(token_ids, trigger, out_grad[0], hidden_acts[0], aggregate_prev[0], stale[0])

time: 90.4 us -> 86 us (0.951)
  Pallas kernels: 85.6 us -> 81.2 us
    pallas_call x1, Pallas kernels: 85.6 us -> 81.2 us  [local(): pl.pallas_call(functools.partial(reduce_kernel, rows, cols), out_shape=(j...]
where the time goes in v3:
time: 86 us; the launch traced here: 85.8 us
  Pallas kernels  81.2 us (94%)
  between operations  2.35 us (3%)
  other arithmetic  2.19 us (3%)
    pallas_call x1, Pallas kernels, local(): pl.pallas_call(functools.partial(reduce_kernel, rows, cols), out_shape=(j...  81.2 us
    broadcast_in_dim x1, other arithmetic, local(): return (aggregate[None], (aggregate * factor)[None], count[0, 0])  2.19 us

profile of v3, /device:TPU:1, one launch (start us, length us, event | category | flops | bytes accessed | tf_op | source)
XLA Modules:
  0.0 85.8 jit_solution(3654876595917941342)
XLA Ops:
  0.6 0.0 copy-start
  0.6 81.2 %reduce_deltas.1 = (f32[16,1024]{1,0:T(8,128)}, f32[1,1]{1,0:T(1,128)}, f32[1,1]{1,0:T(1,128)}) custom-call(s32[1,128]{1,0:T(1,128)} %ids_hbm.1, s32[1,128]{1,0:T(1,128)} %trigger_hbm.1, bf16[128,1024]{1,0:T(8,128)(2,1)} %bitcast.15, bf16[128,2048]{1,0:T(8,128)(2,1)} %bitcast.13, f32[16,1024]{1,0:T(8,128)} %bitcast.14, bf16[2048,1024]{1,0:T(8,128)(2,1)} %bitcast.12), custom_call_target="tpu_custom_call" | custom-call | tf_op jit(solution)/shard_map/reduce_deltas/pallas_call | solution.py:309
  81.9 0.0 copy-done
  81.9 2.2 %multiply_bitcast_fusion = (f32[1,16,1024]{2,1,0:T(8,128)}, f32[1,16,1024]{2,1,0:T(8,128)}) fusion(f32[]{:T(128)} %bitcast.5, f32[16,1024]{1,0:T(8,128)} %get-tuple-element.6, f32[1,16,1024]{2,1,0:T(8,128)S(1)} %copy-done), kind=kLoop, calls=%fused_computation | loop fusion | flops 32768 | bytes 262148 | tf_op jit(solution)/shard_map/broadcast_in_dim | solution.py:358
Async XLA Ops:
  0.6 81.3 %copy-start = (f32[1,16,1024]{2,1,0:T(8,128)S(1)}, f32[1,16,1024]{2,1,0:T(8,128)}, u32[]{:S(2)}) copy-start(f32[1,16,1024]{2,1,0:T(8,128)} %param.11) | copy-start | bytes 196612

commit v4 on v3

--- a/solution.py
+++ b/solution.py
@@ -11,6 +11,9 @@
 NY, NX, NZ = 4, 2, 16
 NG = 2 * NX
 CHUNKS = 8
+EVERY = 4
+X_FIRST = CHUNKS // EVERY
+LEAD = 2
 MESH = pl.DeviceIdType.MESH
 
 clip_ratio = 0.25
@@ -22,9 +25,9 @@
     ids_hbm, trigger_hbm, grad_hbm, hidden_hbm, prev_hbm, stale_hbm,
     total_hbm, factor_ref, count_ref,
     ids_ref, trigger_ref, grad_ref, hidden_ref, prev_ref,
-    total_ref, hidden_t, masked, keep, flags, delta, y_recv, x_data, x_recv, z_data, z_mid, z_recv, squares,
+    total_ref, hidden_t, masked, keep, flags, delta, y_recv, x_data, x_recv, pair_recv, z_data, z_mid, z_recv, squares,
     n_data, n_recv_z, n_recv_p,
-    input_sem, stale_sem, y_send_sem, y_recv_sem, x_send_sem, x_recv_sem, z_send_sem, z_recv_sem,
+    input_sem, stale_sem, y_send_sem, y_recv_sem, x_send_sem, x_recv_sem, pair_sem, z_send_sem, z_recv_sem,
     n_send_sem, n_recv_sem, word_sem,
 ):
     tokens = hidden_ref.shape[0]
@@ -75,8 +78,8 @@
 
     for copy in moves[:4]:
         copy.start()
-    stale_copy(0).start()
-    stale_copy(1).start()
+    for c in (0, EVERY - 1, 1):
+        stale_copy(c).start()
 
     barrier = pltpu.get_barrier_semaphore()
     near = [right, left, across, at(y, x, z_off(1)), at(y, x, z_off(-1))]
@@ -122,20 +125,20 @@
             device_id=across, device_id_type=MESH,
         )
 
+    z_messages = (
+        (-8, -2, 0, None), (-7, -1, 0, None), (7, 1, 0, None),
+        (-5, -2, 1, None), (-4, -1, 1, None), (None, -3, 1, 0),
+        (5, 2, 1, None), (4, 1, 1, None), (None, 3, 1, 1),
+        (-2, -2, 2, None), (-1, -1, 2, None), (None, -3, 2, 2),
+        (2, 2, 2, None), (1, 1, 2, None), (None, 3, 2, 3),
+    )
+
     def z_copy(c, m):
-        if m < 4:
-            source, to = z_data.at[c, z_off(-(m + 5))], -(m + 1)
-        elif m < 7:
-            source, to = z_data.at[c, z_off(m + 1)], m - 3
-        elif m < 9:
-            source, to = z_mid.at[c, m - 7], (-4, 4)[m - 7]
-        elif m < 12:
-            source, to = z_data.at[c, z_off(-(m - 8))], -(m - 8)
-        else:
-            source, to = z_data.at[c, z_off(m - 11)], m - 11
-        return pltpu.make_async_remote_copy(
-            source, z_recv.at[c, m], z_send_sem.at[0], z_recv_sem.at[c, 0 if m < 7 else 1],
-            device_id=at(y, x, z_off(to)), device_id_type=MESH,
+        k, hops, batch, middle = z_messages[m]
+        source = z_data.at[c, z_off(k)] if middle is None else z_mid.at[c, middle]
+        return pltpu.make_async_remote_copy(
+            source, z_recv.at[c, m], z_send_sem.at[0], z_recv_sem.at[c, batch],
+            device_id=at(y, x, z_off(hops)), device_id_type=MESH,
         )
 
     def arrived(ref, sem):
@@ -157,15 +160,13 @@
                 flag * diff[i * BLOCK : (i + 1) * BLOCK]
             ).astype(jnp.bfloat16)
 
-    def begin(c, first=False):
+    def prepare(c):
         part = grad_ref[:, pl.ds(pl.multiple_of(c * width, 128), width)]
         masked[...] = (part.astype(jnp.float32) * keep[...]).astype(jnp.bfloat16)
         stale_copy(c).wait()
 
-        @pl.when(c + 2 < CHUNKS)
-        def _():
-            stale_copy(c + 2).start()
-
+    def begin(c, first=False):
+        prepare(c)
         compute(c, y_far, 0, first)
         compute(c, y_far, 1, first)
         if first:
@@ -200,26 +201,102 @@
             )
         x_copy(c).start()
 
+    def pair_copy(c, yy):
+        return pltpu.make_async_remote_copy(
+            delta.at[c, rows_of(yy, 1 - x)], pair_recv.at[c // EVERY, yy],
+            x_send_sem.at[1], pair_sem.at[c // EVERY],
+            device_id=across, device_id_type=MESH,
+        )
+
+    quarter = half // 2
+
+    def part_of(yy, h):
+        return pl.ds(pl.multiple_of(first_row(yy, x) + h * quarter, quarter), quarter)
+
+    def y_pair_copy(c, m):
+        yy, h, device = (
+            (y_far, 0, left), (y_far, 1, right),
+            (y_left, 1, left), (y_right, 0, right),
+            (y_left, 0, left), (y_right, 1, right),
+        )[m]
+        return pltpu.make_async_remote_copy(
+            delta.at[c, part_of(yy, h)], y_recv.at[c, m, pl.ds(0, quarter)],
+            y_send_sem.at[0], y_recv_sem.at[c, min(m, 2)],
+            device_id=device, device_id_type=MESH,
+        )
+
+    def begin_pair(c):
+        prepare(c)
+        for yy in range(NY):
+            compute(c, yy, 1 - x, False)
+            if yy > 0:
+                pair_copy(c, yy - 1).start()
+        compute(c, 0, x, False)
+        pair_copy(c, NY - 1).start()
+        for yy in range(1, NY):
+            compute(c, yy, x, False)
+
+    def sum_pair(c):
+        arrived(pair_recv.at[c // EVERY], pair_sem.at[c // EVERY])
+
+        def both(yy):
+            return delta[c, rows_of(yy, x), :].astype(jnp.float32) + pair_recv[c // EVERY, yy].astype(jnp.float32)
+
+        for yy in (y_far, y_left, y_right):
+            delta[c, rows_of(yy, x), :] = both(yy).astype(jnp.bfloat16)
+        for m in range(4):
+            y_pair_copy(c, m).start()
+        x_data[c, 0] = both(y)
+
+    def pass_on_pair(c):
+        for m, yy, h in ((0, y_left, 0), (1, y_right, 1)):
+            y_pair_copy(c, m).wait_recv()
+            where = part_of(yy, h)
+            total = delta[c, where, :].astype(jnp.float32) + y_recv[c, m, pl.ds(0, quarter), :].astype(jnp.float32)
+            delta[c, where, :] = total.astype(jnp.bfloat16)
+            y_pair_copy(c, m + 4).start()
+
+    def send_z(c):
+        for m in (0, 2, 1, 3, 6, 4, 7, 9, 12, 10, 13):
+            z_copy(c, m).start()
+
+    def sum_y_pair(c):
+        arrived(y_recv.at[c, pl.ds(2, 2)], y_recv_sem.at[c, 2])
+        for h, first, second in ((0, 3, 4), (1, 2, 5)):
+            for k in range(NZ // 2):
+                part = pl.ds(k * own, own)
+                z_data[c, h * (NZ // 2) + k] = (
+                    x_data[c, 0, pl.ds(h * quarter + k * own, own), :]
+                    + y_recv[c, first, part, :].astype(jnp.float32)
+                    + y_recv[c, second, part, :].astype(jnp.float32)
+                )
+        send_z(c)
+
     def sum_x(c):
         x_copy(c).wait_recv()
         for k in range(NZ):
             part = pl.ds(k * own, own)
             z_data[c, k] = x_data[c, x, part, :] + x_recv[c, part, :]
-        for m in (3, 2, 1, 0, 6, 5, 4, 11, 10, 9, 14, 13, 12):
-            z_copy(c, m).start()
+        send_z(c)
 
     def pass_on_z(c):
-        arrived(z_recv.at[c, pl.ds(0, 7)], z_recv_sem.at[c, 0])
-        low = z_data[c, z_off(-4)] + z_recv[c, 0] + z_recv[c, 1]
-        z_mid[c, 0] = low + z_recv[c, 2] + z_recv[c, 3]
-        z_copy(c, 7).start()
-        z_mid[c, 1] = z_data[c, z_off(4)] + z_recv[c, 4] + z_recv[c, 5] + z_recv[c, 6]
+        arrived(z_recv.at[c, pl.ds(0, 3)], z_recv_sem.at[c, 0])
+        z_mid[c, 0] = z_data[c, z_off(-6)] + z_recv[c, 0] + z_recv[c, 1]
+        z_copy(c, 5).start()
+        z_mid[c, 1] = z_data[c, z_off(6)] + z_recv[c, 2]
         z_copy(c, 8).start()
 
+    def pass_on_again(c):
+        arrived(z_recv.at[c, pl.ds(3, 6)], z_recv_sem.at[c, 1])
+        z_mid[c, 2] = z_data[c, z_off(-3)] + z_recv[c, 3] + z_recv[c, 4] + z_recv[c, 5]
+        z_copy(c, 11).start()
+        z_mid[c, 3] = z_data[c, z_off(3)] + z_recv[c, 6] + z_recv[c, 7] + z_recv[c, 8]
+        z_copy(c, 14).start()
+
     def finish(c):
-        arrived(z_recv.at[c, pl.ds(7, 8)], z_recv_sem.at[c, 1])
+        arrived(z_recv.at[c, pl.ds(9, 6)], z_recv_sem.at[c, 2])
         total = z_data[c, z]
-        for m in range(7, 15):
+        for m in range(9, 15):
             total = total + z_recv[c, m]
         where = pl.ds(pl.multiple_of(c * width, 128), width)
         total_ref[:, where] = total
@@ -229,29 +306,49 @@
     moves[2].wait()
     moves[3].wait()
     begin(0, first=True)
+    for c in range(CHUNKS):
+        if c not in (0, EVERY - 1, 1):
+            stale_copy(c).start()
     moves[4].start()
 
-    @pl.loop(1, CHUNKS + 5)
+    @pl.loop(1, CHUNKS + 8)
     def _(s):
-        @pl.when(s < CHUNKS)
+        def stage(lag, run, x_first):
+            c = s - lag
+            fits = (c % EVERY == EVERY - 1) if x_first else (c % EVERY != EVERY - 1)
+
+            @pl.when((c >= 0) & (c < CHUNKS) & fits)
+            def _():
+                run(c)
+
+        stage(0, begin, False)
+        stage(0, sum_pair, True)
+
+        @pl.when((s + LEAD < CHUNKS) & ((s + LEAD) % EVERY == EVERY - 1))
         def _():
-            begin(s)
-
-        for i in range(3):
+            begin_pair(s + LEAD)
+
+        for i in range(2):
 
             @pl.when(s == i + 1)
             def _(i=i):
                 pl.semaphore_wait(word_sem.at[i], 2)
-                if i < 2:
+                if i < 1:
                     tell_z(i + 1)
                 else:
                     moves[4].wait()
 
-        for lag, stage in enumerate((pass_on, sum_y, sum_x, pass_on_z, finish), 1):
-
-            @pl.when((s >= lag) & (s < CHUNKS + lag))
-            def _(lag=lag, stage=stage):
-                stage(s - lag)
+        stage(1, pass_on, False)
+        stage(1, pass_on_pair, True)
+        stage(2, sum_y, False)
+        stage(2, sum_y_pair, True)
+        stage(3, sum_x, False)
+        stage(3, pass_on_z, True)
+        stage(4, pass_on_z, False)
+        stage(5, pass_on_again, True)
+        stage(6, pass_on_again, False)
+        stage(7, finish, True)
+        stage(8, finish, False)
 
     lanes = squares[0:8, 0:128]
     for i in range(own // 8):
@@ -277,8 +374,9 @@
     for k in (8, 7, 9, 6, 10, 5, 11, 4, 12, 3, 13, 2, 14, 1, 15):
         n_copy(k).start()
     moves[5].start()
-    arrived(y_recv, y_send_sem.at[0])
-    arrived(x_recv, x_send_sem.at[0])
+    arrived(y_recv.at[pl.ds(0, CHUNKS - X_FIRST // 2)], y_send_sem.at[0])
+    arrived(x_recv.at[pl.ds(0, CHUNKS - X_FIRST)], x_send_sem.at[0])
+    arrived(pair_recv, x_send_sem.at[1])
     arrived(z_recv, z_send_sem.at[0])
     arrived(n_recv_z, n_recv_sem.at[0])
     n_data[1] = n_data[0] + jnp.sum(n_recv_z[...], axis=0)
@@ -330,8 +428,9 @@
             pltpu.VMEM((CHUNKS, 6, half, width), bf16),
             pltpu.VMEM((CHUNKS, NX, half, width), f32),
             pltpu.VMEM((CHUNKS, half, width), f32),
+            pltpu.VMEM((X_FIRST, NY, half, width), bf16),
             pltpu.VMEM((CHUNKS, NZ, own, width), f32),
-            pltpu.VMEM((CHUNKS, 2, own, width), f32),
+            pltpu.VMEM((CHUNKS, 4, own, width), f32),
             pltpu.VMEM((CHUNKS, 15, own, width), f32),
             pltpu.VMEM((own, width), f32),
             pltpu.VMEM((2, 2, 128), f32),
@@ -341,13 +440,14 @@
             dma((CHUNKS,)),
             dma((1,)),
             dma((CHUNKS, 3)),
+            dma((2,)),
+            dma((CHUNKS,)),
+            dma((X_FIRST,)),
             dma((1,)),
-            dma((CHUNKS,)),
-            dma((1,)),
-            dma((CHUNKS, 2)),
+            dma((CHUNKS, 3)),
             dma((2,)),
             dma((2,)),
-            pltpu.SemaphoreType.REGULAR((3,)),
+            pltpu.SemaphoreType.REGULAR((2,)),
         ],
         compiler_params=pltpu.CompilerParams(
             collective_id=0, has_side_effects=True, vmem_limit_bytes=66_900_000

time: 86 us -> 82.8 us (0.963)
  Pallas kernels: 81.2 us -> 78 us
    pallas_call x1, Pallas kernels: 81.2 us -> 78 us  [local(): pl.pallas_call(functools.partial(reduce_kernel, rows, cols), out_shape=(j...]
where the time goes in v4:
time: 82.8 us; the launch traced here: 82.5 us
  Pallas kernels  78 us (94%)
  between operations  2.35 us (3%)
  other arithmetic  2.19 us (3%)
    pallas_call x1, Pallas kernels, local(): pl.pallas_call(functools.partial(reduce_kernel, rows, cols), out_shape=(j...  78 us
    broadcast_in_dim x1, other arithmetic, local(): return (aggregate[None], (aggregate * factor)[None], count[0, 0])  2.19 us

profile of v4, /device:TPU:1, one launch (start us, length us, event | category | flops | bytes accessed | tf_op | source)
XLA Modules:
  0.0 82.5 jit_solution(6907686782227868624)
XLA Ops:
  0.6 0.0 copy-start
  0.6 78.0 %reduce_deltas.1 = (f32[16,1024]{1,0:T(8,128)}, f32[1,1]{1,0:T(1,128)}, f32[1,1]{1,0:T(1,128)}) custom-call(s32[1,128]{1,0:T(1,128)} %ids_hbm.1, s32[1,128]{1,0:T(1,128)} %trigger_hbm.1, bf16[128,1024]{1,0:T(8,128)(2,1)} %bitcast.15, bf16[128,2048]{1,0:T(8,128)(2,1)} %bitcast.13, f32[16,1024]{1,0:T(8,128)} %bitcast.14, bf16[2048,1024]{1,0:T(8,128)(2,1)} %bitcast.12), custom_call_target="tpu_custom_call" | custom-call | tf_op jit(solution)/shard_map/reduce_deltas/pallas_call | solution.py:407
  78.6 0.0 copy-done
  78.6 2.2 %multiply_bitcast_fusion = (f32[1,16,1024]{2,1,0:T(8,128)}, f32[1,16,1024]{2,1,0:T(8,128)}) fusion(f32[]{:T(128)} %bitcast.5, f32[16,1024]{1,0:T(8,128)} %get-tuple-element.6, f32[1,16,1024]{2,1,0:T(8,128)S(1)} %copy-done), kind=kLoop, calls=%fused_computation | loop fusion | flops 32768 | bytes 262148 | tf_op jit(solution)/shard_map/broadcast_in_dim | solution.py:458
Async XLA Ops:
  0.6 78.0 %copy-start = (f32[1,16,1024]{2,1,0:T(8,128)S(1)}, f32[1,16,1024]{2,1,0:T(8,128)}, u32[]{:S(2)}) copy-start(f32[1,16,1024]{2,1,0:T(8,128)} %param.11) | copy-start | bytes 196612

commit v5 on v4

--- a/solution.py
+++ b/solution.py
@@ -392,6 +392,36 @@
     count_ref[...] = jnp.sum(both[1:2, :], axis=1, keepdims=True)
 
     arrived(n_recv_p, n_send_sem.at[1])
+
+
+def output_kernel(
+    total_hbm, prev_hbm, factor_hbm, count_hbm, aggregate_hbm, update_hbm, triggered_hbm,
+    total, prev, factor, count, update, sems,
+):
+    loads = [
+        pltpu.make_async_copy(source, target, sems.at[i])
+        for i, (source, target) in enumerate(
+            ((total_hbm, total), (prev_hbm, prev), (factor_hbm, factor), (count_hbm, count))
+        )
+    ]
+    stores = [
+        pltpu.make_async_copy(source, target, sems.at[4 + i])
+        for i, (source, target) in enumerate(
+            ((total, aggregate_hbm), (update, update_hbm), (count, triggered_hbm))
+        )
+    ]
+    for copy in loads:
+        copy.start()
+    for copy in loads:
+        copy.wait()
+    stores[2].start()
+    aggregate = prev[...] + total[...]
+    update[...] = aggregate * factor[...]
+    total[...] = aggregate
+    stores[1].start()
+    stores[0].start()
+    for copy in stores:
+        copy.wait()
 
 
 def local(hidden_acts, out_grad, token_ids, trigger, stale, aggregate_prev):
@@ -454,8 +484,27 @@
         ),
         name="reduce_deltas",
     )(token_ids, trigger, out_grad[0], hidden_acts[0], aggregate_prev[0], stale[0])
-    aggregate = aggregate_prev[0] + total
-    return (aggregate[None], (aggregate * factor)[None], count[0, 0])
+    aggregate, update, triggered = pl.pallas_call(
+        output_kernel,
+        out_shape=(
+            jax.ShapeDtypeStruct((own, cols), f32),
+            jax.ShapeDtypeStruct((own, cols), f32),
+            jax.ShapeDtypeStruct((1, 1), f32),
+        ),
+        in_specs=[hbm] * 4,
+        out_specs=(hbm,) * 3,
+        scratch_shapes=[
+            pltpu.VMEM((own, cols), f32),
+            pltpu.VMEM((own, cols), f32),
+            pltpu.VMEM((1, 1), f32),
+            pltpu.VMEM((1, 1), f32),
+            pltpu.VMEM((own, cols), f32),
+            dma((7,)),
+        ],
+        compiler_params=pltpu.CompilerParams(vmem_limit_bytes=67_000_000),
+        name="clip",
+    )(total, aggregate_prev[0], factor, count)
+    return (aggregate[None], update[None], triggered[0, 0])
 
 
 def solution(mesh):

time: 82.8 us -> 81.7 us (0.987)
  Pallas kernels: 78 us -> 80.9 us
  other arithmetic: 2.19 us -> 0 us
  between operations: 2.35 us -> 0.64 us
    pallas_call x0 -> x1, Pallas kernels: none -> 2.91 us  [local(): pl.pallas_call(output_kernel, out_shape=(jax.ShapeDtypeStruct((own, cols)...]
    broadcast_in_dim x1 -> x0, other arithmetic: 2.19 us -> none  [local(): return (aggregate[None], (aggregate * factor)[None], count[0, 0])]
where the time goes in v5:
time: 81.7 us; the launch traced here: 81.5 us
  Pallas kernels  80.9 us (99%)
    pallas_call x1, Pallas kernels, local(): pl.pallas_call(functools.partial(reduce_kernel, rows, cols), out_shape=(j...  77.9 us
    pallas_call x1, Pallas kernels, local(): pl.pallas_call(output_kernel, out_shape=(jax.ShapeDtypeStruct((own, cols)...  2.91 us

profile of v5, /device:TPU:1, one launch (start us, length us, event | category | flops | bytes accessed | tf_op | source)
XLA Modules:
  0.0 81.5 jit_solution(188375712626114629)
XLA Ops:
  0.6 77.9 %reduce_deltas.1 = (f32[16,1024]{1,0:T(8,128)}, f32[1,1]{1,0:T(1,128)}, f32[1,1]{1,0:T(1,128)}) custom-call(s32[1,128]{1,0:T(1,128)} %ids_hbm.1, s32[1,128]{1,0:T(1,128)} %trigger_hbm.1, bf16[128,1024]{1,0:T(8,128)(2,1)} %bitcast.11, bf16[128,2048]{1,0:T(8,128)(2,1)} %bitcast.8, f32[16,1024]{1,0:T(8,128)} %bitcast.9, bf16[2048,1024]{1,0:T(8,128)(2,1)} %bitcast.7), custom_call_target="tpu_custom_call" | custom-call | tf_op jit(solution)/shard_map/reduce_deltas/pallas_call | solution.py:437
  78.6 2.9 %clip.1 = (f32[16,1024]{1,0:T(8,128)}, f32[16,1024]{1,0:T(8,128)}, f32[1,1]{1,0:T(1,128)}) custom-call(f32[16,1024]{1,0:T(8,128)} %get-tuple-element.9.total_hbm, f32[16,1024]{1,0:T(8,128)} %bitcast.10, f32[1,1]{1,0:T(1,128)} %get-tuple-element.10.factor_hbm, f32[1,1]{1,0:T(1,128)} %get-tuple-element.11.count_hbm), custom_call_target="tpu_custom_call" | custom-call | tf_op jit(solution)/shard_map/clip/pallas_call | solution.py:487

commit v6 on v5

--- a/solution.py
+++ b/solution.py
@@ -78,8 +78,7 @@
 
     for copy in moves[:4]:
         copy.start()
-    for c in (0, EVERY - 1, 1):
-        stale_copy(c).start()
+    stale_copy(0).start()
 
     barrier = pltpu.get_barrier_semaphore()
     near = [right, left, across, at(y, x, z_off(1)), at(y, x, z_off(-1))]
@@ -167,6 +166,9 @@
 
     def begin(c, first=False):
         prepare(c)
+        if first:
+            for later in sorted(range(1, CHUNKS), key=lambda k: (k > 1, k != EVERY - 1)):
+                stale_copy(later).start()
         compute(c, y_far, 0, first)
         compute(c, y_far, 1, first)
         if first:
@@ -306,12 +308,9 @@
     moves[2].wait()
     moves[3].wait()
     begin(0, first=True)
-    for c in range(CHUNKS):
-        if c not in (0, EVERY - 1, 1):
-            stale_copy(c).start()
     moves[4].start()
 
-    @pl.loop(1, CHUNKS + 8)
+    @pl.loop(1, CHUNKS + 9)
     def _(s):
         def stage(lag, run, x_first):
             c = s - lag
@@ -342,13 +341,13 @@
         stage(1, pass_on_pair, True)
         stage(2, sum_y, False)
         stage(2, sum_y_pair, True)
-        stage(3, sum_x, False)
+        stage(4, sum_x, False)
         stage(3, pass_on_z, True)
-        stage(4, pass_on_z, False)
+        stage(5, pass_on_z, False)
         stage(5, pass_on_again, True)
-        stage(6, pass_on_again, False)
+        stage(7, pass_on_again, False)
         stage(7, finish, True)
-        stage(8, finish, False)
+        stage(9, finish, False)
 
     lanes = squares[0:8, 0:128]
     for i in range(own // 8):

time: 81.7 us -> 81.1 us (level)
  no operation moved by 1% of the time
where the time goes in v6:
time: 81.1 us; the launch traced here: 80.9 us
  Pallas kernels  80.3 us (99%)
    pallas_call x1, Pallas kernels, local(): pl.pallas_call(functools.partial(reduce_kernel, rows, cols), out_shape=(j...  77.4 us
    pallas_call x1, Pallas kernels, local(): pl.pallas_call(output_kernel, out_shape=(jax.ShapeDtypeStruct((own, cols)...  2.91 us

profile of v6, /device:TPU:1, one launch (start us, length us, event | category | flops | bytes accessed | tf_op | source)
XLA Modules:
  0.0 80.9 jit_solution(7569772270192289895)
XLA Ops:
  0.6 77.4 %reduce_deltas.1 = (f32[16,1024]{1,0:T(8,128)}, f32[1,1]{1,0:T(1,128)}, f32[1,1]{1,0:T(1,128)}) custom-call(s32[1,128]{1,0:T(1,128)} %ids_hbm.1, s32[1,128]{1,0:T(1,128)} %trigger_hbm.1, bf16[128,1024]{1,0:T(8,128)(2,1)} %bitcast.11, bf16[128,2048]{1,0:T(8,128)(2,1)} %bitcast.8, f32[16,1024]{1,0:T(8,128)} %bitcast.9, bf16[2048,1024]{1,0:T(8,128)(2,1)} %bitcast.7), custom_call_target="tpu_custom_call" | custom-call | tf_op jit(solution)/shard_map/reduce_deltas/pallas_call | solution.py:436
  78.0 2.9 %clip.1 = (f32[16,1024]{1,0:T(8,128)}, f32[16,1024]{1,0:T(8,128)}, f32[1,1]{1,0:T(1,128)}) custom-call(f32[16,1024]{1,0:T(8,128)} %get-tuple-element.9.total_hbm, f32[16,1024]{1,0:T(8,128)} %bitcast.10, f32[1,1]{1,0:T(1,128)} %get-tuple-element.10.factor_hbm, f32[1,1]{1,0:T(1,128)} %get-tuple-element.11.count_hbm), custom_call_target="tpu_custom_call" | custom-call | tf_op jit(solution)/shard_map/clip/pallas_call | solution.py:486
